TPU v7x, 32 devices: a whole 2x2x4 slice. The times are simulated.
32 devices in a mesh: pb: 4 (over x, core), db: 8 (over z, y).
Axes of the slice: x: 2, y: 2, z: 4, core: 2. Of those that a mesh axis runs over, the one named last changes fastest.
Arguments:
- queries: bfloat16 [128, 1024], P(('pb', 'db')), may hold values from -6 to 6
- residual: bfloat16 [8192, 1024], P('db'), may hold values from -3 to 3
- codes: int32 [8192, 64], P('db'), may hold values from 0 to 255
- codebook: float32 [64, 256, 16], replicated, may hold values from -6 to 6
- ranks: int32 [128], P(('pb', 'db')), may hold values from 0 to 63
Outputs:
- hits: float32 [3, 128], P(None, ('pb', 'db'))
- totals: float32 [3], replicated
All inputs are finite; a program needn't handle non-finite values.
Results may differ from a plain program's by a relative error of at most 0.00035.
Values may be sent and summed in bfloat16 or wider, within the bound.
No kernel may reach another device: no remote copies, remote signals or barrier semaphores. Data moves between devices by JAX's collectives and lax.ppermute only.
A program may use at most 128 MiB of HBM per device.

v0:
```python
import jax
import jax.numpy as jnp
from jax import lax
from jax.sharding import PartitionSpec as P

LEVELS = 64


def pq_lookup(queries, centre_high, centre_low, centre_norms):
    count = queries.shape[0]
    subspaces, centroids, subdim = centre_high.shape
    size = 64 if count % 64 == 0 else count

    def one_group(group):
        parts = group.reshape(size, subspaces, subdim)
        query_parts = jnp.sum(parts.astype(jnp.float32) ** 2, axis=-1)
        cross = jnp.einsum("qmj,mcj->qmc", parts, centre_high, preferred_element_type=jnp.float32)
        cross = cross + jnp.einsum(
            "qmj,mcj->qmc", parts, centre_low, preferred_element_type=jnp.float32
        )
        lookup = (query_parts[:, :, None] + centre_norms[None] - 2.0 * cross) / (subspaces * subdim)
        return lookup.astype(jnp.bfloat16).reshape(size, subspaces * centroids)

    tables = lax.map(one_group, queries.reshape(count // size, size, queries.shape[1]))
    return tables.reshape(count, subspaces * centroids)


def block_hits(queries, query_norms, lookup, bounds, vectors, code_values, centroids):
    width = vectors.shape[1]
    size = vectors.shape[0]
    vector_norms = jnp.sum(vectors.astype(jnp.float32) ** 2, axis=1)
    cross = lax.dot_general(
        queries, vectors, (((1,), (1,)), ((), ())), preferred_element_type=jnp.float32
    )
    exact = (query_norms[:, None] + vector_norms[None, :] - 2.0 * cross) / width
    levels = jnp.arange(centroids, dtype=jnp.bfloat16)
    one_hot = (code_values[:, :, None] == levels).astype(jnp.bfloat16).reshape(size, -1)
    coarse = lax.dot_general(
        lookup, one_hot, (((1,), (1,)), ((), ())), preferred_element_type=jnp.float32
    )
    exact_hit = jax.nn.sigmoid((bounds[:, None] - exact) / 0.02)
    coarse_hit = jax.nn.sigmoid((bounds[:, None] - coarse) / 0.02)
    return jnp.stack(
        [jnp.sum(exact_hit, 1), jnp.sum(coarse_hit, 1), jnp.sum(exact_hit * coarse_hit, 1)]
    )


def sweep(counts, vectors, code_values, queries, query_norms, lookup, bounds, centroids):
    total = vectors.shape[0]
    size = 128
    blocks = total // size
    vector_blocks = vectors.reshape(blocks, size, vectors.shape[1])
    code_blocks = code_values.reshape(blocks, size, code_values.shape[1])

    def absorb_block(carry, item):
        return (
            carry + block_hits(queries, query_norms, lookup, bounds, item[0], item[1], centroids),
            None,
        )

    counts, _ = lax.scan(absorb_block, counts, (vector_blocks, code_blocks))
    return counts


def per_device(queries, residual, codes, codebook, ranks):
    count = queries.shape[0]
    rows_count = residual.shape[0]
    centroids = codebook.shape[1]
    centre_ids = jnp.arange(centroids, dtype=jnp.int32)
    selector = (codes[:, :, None] == centre_ids).astype(jnp.float32)
    recon = jnp.einsum("rmc,mcj->rmj", selector, codebook, precision=lax.Precision.HIGHEST).reshape(
        rows_count, -1
    )
    vectors = (recon + residual.astype(jnp.float32)).astype(jnp.bfloat16)
    code_values = codes.astype(jnp.bfloat16)
    rank_values = ranks.astype(jnp.bfloat16)
    centre_high = codebook.astype(jnp.bfloat16)
    centre_low = (codebook - centre_high.astype(jnp.float32)).astype(jnp.bfloat16)
    centre_norms = jnp.sum(codebook * codebook, axis=-1)
    visiting, visiting_ranks = (
        lax.all_gather(queries, "db", axis=0, tiled=True),
        lax.all_gather(rank_values, "db", axis=0, tiled=True),
    )
    lookup = pq_lookup(visiting, centre_high, centre_low, centre_norms)
    bounds = 1.9 + 0.6 * visiting_ranks.astype(jnp.float32) / (LEVELS - 1)
    visiting_norms = jnp.sum(visiting.astype(jnp.float32) ** 2, axis=1)
    empty = jnp.zeros((3, visiting.shape[0]), jnp.float32)
    partial_value = sweep(
        empty, vectors, code_values, visiting, visiting_norms, lookup, bounds, centroids
    )
    database = rows_count * lax.axis_size("db")
    everyone = count * lax.axis_size("pb") * lax.axis_size("db")
    hits = lax.psum_scatter(partial_value, "db", scatter_dimension=1, tiled=True) / database
    totals = lax.psum(jnp.sum(hits, axis=1), ("pb", "db")) / everyone
    return (hits, totals)


def solution(mesh):
    return jax.shard_map(
        per_device,
        mesh=mesh,
        in_specs=(P(("pb", "db"), None), P("db", None), P("db", None), P(), P(("pb", "db"))),
        out_specs=(P(None, ("pb", "db")), P()),
        check_vma=False,
    )
```

profile of v0, /device:TPU:0, one launch (start us, length us, event | category | flops | bytes accessed | tf_op | source)
XLA Modules:
  0.0 214.8 jit_solution(14085846620095008652)
XLA Ops:
  0.6 32.7 %all-gather = bf16[8,4,1024]{2,1,0:T(4,128)(2,1)S(1)} all-gather(bf16[1,4,1024]{2,1,0:T(4,128)(2,1)} %bitcast.99), channel_id=1, replica_groups=mesh['pb'=4,'db'=8] {'db'}, dimensions={0}, use_global_device_ids=true | all-gather | bytes 73728 | tf_op jit(solution)/shard_map/all_gather | solution.py:81
  39.7 21.3 %all-reduce = bf16[32]{0:T(256)(128)(2,1)S(1)} all-reduce(bf16[32]{0:T(256)(128)(2,1)S(1)} %dynamic-update-slice), channel_id=1, replica_groups=mesh['pb'=4,'db'=8] {'db'}, use_global_device_ids=true, to_apply=%add | all-reduce | flops 32 | bytes 128
  61.1 35.0 %fusion.34 = f32[64,1024,16]{1,2,0:T(8,128)} fusion(f32[64,256,16]{1,2,0:T(8,128)S(1)} %copy-done, s32[1024,64]{0,1:T(8,128)S(1)} %copy-done.3), kind=kOutput, calls=%fused_computation.29 | convolution fusion | flops 3238002688 | bytes 5505024 | tf_op jit(solution)/shard_map/rmc,mcj->rmj/dot_general | solution.py:71
  96.1 5.3 %copy.15 = f32[1024,1024]{1,0:T(8,128)} copy(f32[1024,1024]{0,1:T(8,128)} %bitcast.92) | data formatting | bytes 8388608 | tf_op jit(solution)/shard_map/reshape | solution.py:71
  101.4 3.6 %add_convert_fusion = bf16[1024,1024]{1,0:T(8,128)(2,1)S(1)} fusion(f32[1024,1024]{1,0:T(8,128)} %copy.15, bf16[1024,1024]{1,0:T(8,128)(2,1)} %param.8), kind=kLoop, calls=%fused_computation.31 | loop fusion | flops 3145728 | bytes 8388608 | tf_op jit(solution)/shard_map/convert_element_type | solution.py:74
  105.3 52.1 %while.3 = (s32[]{:T(128)}, f32[3,32]{1,0:T(4,128)S(1)}, f32[32]{0:T(128)S(1)}, f32[32]{0:T(128)S(1)}, bf16[8,128,1024]{2,1,0:T(8,128)(2,1)S(1)}, /*index=5*/bf1...) while((s32[]{:T(128)}, f32[3,32]{1,0:T(4,128)S(1)}, ...), condition=%wide.region_8.9_spmd.clone, body=%wide.region_3.8_spmd.clone.sunk | while | flops 145170592 | bytes 18894612 | solution.py:61
  106.6 2.9 %copy.27 = bf16[16,8,64,256]{3,1,2,0:T(8,128)(2,1)S(1)} copy(bf16[16,8,64,256]{3,2,1,0:T(8,128)(2,1)S(1)} %bitcast.89) | data formatting | bytes 8388608 | tf_op jit(solution)/shard_map/while
  109.6 1.7 fusion.58
  113.1 2.9 %copy.27 = bf16[16,8,64,256]{3,1,2,0:T(8,128)(2,1)S(1)} copy(bf16[16,8,64,256]{3,2,1,0:T(8,128)(2,1)S(1)} %bitcast.89) | data formatting | bytes 8388608 | tf_op jit(solution)/shard_map/while
  116.1 1.7 fusion.58
  119.6 2.9 %copy.27 = bf16[16,8,64,256]{3,1,2,0:T(8,128)(2,1)S(1)} copy(bf16[16,8,64,256]{3,2,1,0:T(8,128)(2,1)S(1)} %bitcast.89) | data formatting | bytes 8388608 | tf_op jit(solution)/shard_map/while
  122.6 1.7 fusion.58
  126.1 2.9 %copy.27 = bf16[16,8,64,256]{3,1,2,0:T(8,128)(2,1)S(1)} copy(bf16[16,8,64,256]{3,2,1,0:T(8,128)(2,1)S(1)} %bitcast.89) | data formatting | bytes 8388608 | tf_op jit(solution)/shard_map/while
  129.1 1.7 fusion.58
  132.6 2.9 %copy.27 = bf16[16,8,64,256]{3,1,2,0:T(8,128)(2,1)S(1)} copy(bf16[16,8,64,256]{3,2,1,0:T(8,128)(2,1)S(1)} %bitcast.89) | data formatting | bytes 8388608 | tf_op jit(solution)/shard_map/while
  135.6 1.7 fusion.58
  139.2 2.9 %copy.27 = bf16[16,8,64,256]{3,1,2,0:T(8,128)(2,1)S(1)} copy(bf16[16,8,64,256]{3,2,1,0:T(8,128)(2,1)S(1)} %bitcast.89) | data formatting | bytes 8388608 | tf_op jit(solution)/shard_map/while
  142.1 1.7 fusion.58
  145.7 2.9 %copy.27 = bf16[16,8,64,256]{3,1,2,0:T(8,128)(2,1)S(1)} copy(bf16[16,8,64,256]{3,2,1,0:T(8,128)(2,1)S(1)} %bitcast.89) | data formatting | bytes 8388608 | tf_op jit(solution)/shard_map/while
  148.7 1.7 fusion.58
  152.2 2.9 %copy.27 = bf16[16,8,64,256]{3,1,2,0:T(8,128)(2,1)S(1)} copy(bf16[16,8,64,256]{3,2,1,0:T(8,128)(2,1)S(1)} %bitcast.89) | data formatting | bytes 8388608 | tf_op jit(solution)/shard_map/while
  155.2 1.7 fusion.58
  157.4 17.1 %all-reduce.1 = f32[3,32]{1,0:T(4,128)S(1)} all-reduce(f32[3,32]{1,0:T(4,128)S(1)} %get-tuple-element.62), channel_id=2, replica_groups=mesh['pb'=4,'db'=8] {'db'}, use_global_device_ids=true, to_apply=%region_9.10.clone | all-reduce | flops 96 | bytes 768
  176.0 38.3 %psum.7 = f32[3]{0:T(128)S(1)} all-reduce(f32[3]{0:T(128)S(1)} %get-tuple-element.108), channel_id=1, replica_groups=mesh['pb'=4,'db'=8] {'pb','db'}, use_global_device_ids=true, to_apply=%region_11.12 | all-reduce | flops 3 | bytes 24 | tf_op jit(solution)/shard_map/psum | solution.py:94
  (106 shorter events, 21.4 us)
Async XLA Ops:
  0.6 34.5 %copy-start = (f32[64,256,16]{1,2,0:T(8,128)S(1)}, f32[64,256,16]{1,2,0:T(8,128)}, u32[]{:S(2)}) copy-start(f32[64,256,16]{1,2,0:T(8,128)} %param.10) | copy-start | bytes 3145732
  33.7 0.8 copy-start.1
  35.1 1.0 copy-start.2
  37.5 0.7 copy-start.6
  37.6 1.9 copy-start.7
  37.6 23.5 %copy-start.3 = (s32[1024,64]{0,1:T(8,128)S(1)}, s32[1024,64]{0,1:T(8,128)}, u32[]{:S(2)}) copy-start(s32[1024,64]{0,1:T(8,128)} %param.9) | copy-start | bytes 786436
  37.7 58.4 %copy-start.4 = (bf16[32,1024]{1,0:T(8,128)(2,1)}, bf16[32,1024]{1,0:T(8,128)(2,1)S(1)}, u32[]{:S(2)}) copy-start(bf16[32,1024]{1,0:T(8,128)(2,1)S(1)} %reshape.48) | copy-start | bytes 196612
  109.6 1.9 copy-start.5
  116.1 1.9 copy-start.5
  122.6 1.9 copy-start.5
  129.1 1.9 copy-start.5
  135.6 1.9 copy-start.5
  142.1 1.9 copy-start.5
  148.6 1.9 copy-start.5
  155.2 1.9 copy-start.5
where the time goes:
time: 216 us; the launch traced here: 215 us
  blocking collectives  109 us (50%)
  matrix products  52.8 us (24%)
  local copies, waits for them, and re-layouts  43 us (20%)
  other arithmetic  6.92 us (3%)
    unnamed x2, blocking collectives  38.5 us
    psum x1, blocking collectives, per_device(): totals = lax.psum(jnp.sum(hits, axis=1), ('pb', 'db')) / everyone  38.3 us
    dot_general x1, matrix products, per_device(): jnp.einsum('rmc,mcj->rmj', selector, codebook, precision=lax.Precision.HI...  35 us
    all_gather x1, blocking collectives, per_device(): lax.all_gather(queries, 'db', axis=0, tiled=True)  32.7 us
    while x40, local copies, waits for them, and re-layouts  23.7 us
    dot_general x8, matrix products, block_hits(): lax.dot_general(lookup, one_hot, (((1,), (1,)), ((), ())), preferred_elem...  13.9 us
    eq x16, local copies, waits for them, and re-layouts, block_hits(): code_values[:, :, None] == levels  10 us
    reshape x1, local copies, waits for them, and re-layouts, per_device(): jnp.einsum('rmc,mcj->rmj', selector, codebook, precision=lax.Precision.HI...  5.34 us

commit v1 on v0

v1 whole, which is shorter than its diff:
```python
import functools

import jax
import jax.numpy as jnp
from jax import lax
from jax.experimental import pallas as pl
from jax.experimental.pallas import tpu as pltpu
from jax.sharding import PartitionSpec as P

LEVELS = 64
LANES = 128


def build_kernel(codes_ref, codebook_ref, residual_ref, recon_ref, vectors_ref, norms_ref):
    subspaces, subdim, centroids = codebook_ref.shape
    rows = codes_ref.shape[1]

    @pl.when(pl.program_id(0) == 0)
    def _():
        norms_ref[...] = jnp.zeros_like(norms_ref)

    def one_tile(tile, _):
        at = pl.ds(pl.multiple_of(tile * LANES, LANES), LANES)
        residual = residual_ref[at, :].astype(jnp.float32).T
        recon_norm = jnp.zeros((subdim, LANES), jnp.float32)
        vector_norm = jnp.zeros((subdim, LANES), jnp.float32)
        for m in range(subspaces):
            code = jnp.broadcast_to(codes_ref[m : m + 1, at], (subdim, LANES))
            lane = code % LANES
            recon = jnp.zeros((subdim, LANES), jnp.float32)
            for part in range(centroids // LANES):
                table = codebook_ref[m, :, part * LANES : (part + 1) * LANES]
                picked = jnp.take_along_axis(table, lane, axis=1, mode="promise_in_bounds")
                recon = jnp.where(code // LANES == part, picked, recon)
            features = slice(m * subdim, (m + 1) * subdim)
            vector = (recon + residual[features]).astype(jnp.bfloat16)
            wide = vector.astype(jnp.float32)
            recon_norm += recon * recon
            vector_norm += wide * wide
            recon_ref[features, at] = recon.astype(jnp.bfloat16)
            vectors_ref[features, at] = vector
        norms_ref[0:1, at] += jnp.sum(vector_norm, axis=0, keepdims=True)
        norms_ref[1:2, at] += jnp.sum(recon_norm, axis=0, keepdims=True)
        return 0

    lax.fori_loop(0, rows // LANES, one_tile, 0)


def build(codes, codebook, residual):
    subspaces, subdim, centroids = codebook.shape
    rows, width = residual.shape
    group = LANES // subdim
    return pl.pallas_call(
        build_kernel,
        grid=(subspaces // group,),
        in_specs=[
            pl.BlockSpec((group, rows), lambda g: (g, 0)),
            pl.BlockSpec((group, subdim, centroids), lambda g: (g, 0, 0)),
            pl.BlockSpec((rows, LANES), lambda g: (0, g)),
        ],
        out_specs=[
            pl.BlockSpec((LANES, rows), lambda g: (g, 0)),
            pl.BlockSpec((LANES, rows), lambda g: (g, 0)),
            pl.BlockSpec((8, rows), lambda g: (0, 0)),
        ],
        out_shape=[
            jax.ShapeDtypeStruct((width, rows), jnp.bfloat16),
            jax.ShapeDtypeStruct((width, rows), jnp.bfloat16),
            jax.ShapeDtypeStruct((8, rows), jnp.float32),
        ],
        compiler_params=pltpu.CompilerParams(
            dimension_semantics=("arbitrary",), vmem_limit_bytes=8 * 2**20
        ),
        cost_estimate=pl.CostEstimate(
            flops=32 * rows * width, bytes_accessed=8 * rows * width, transcendentals=0
        ),
        name="build",
    )(codes, codebook, residual)


def count_kernel(visiting_ref, recon_ref, vectors_ref, norms_ref, out_ref, gathered):
    senders, count, packed = visiting_ref.shape
    width = recon_ref.shape[0]
    for s in range(senders):
        gathered[s * count : (s + 1) * count, :] = visiting_ref[s].astype(jnp.float32)
    queries = gathered[:, :width]
    query_norms = jnp.sum(queries * queries, axis=1, keepdims=True)
    bounds = 1.9 + 0.6 * gathered[:, width : width + 1] / (LEVELS - 1)
    queries = queries.astype(jnp.bfloat16)

    def hit(values_ref, norms):
        cross = jnp.dot(queries, values_ref[...], preferred_element_type=jnp.float32)
        distance = (query_norms + norms - 2.0 * cross) / width
        return jax.nn.sigmoid((bounds - distance) / 0.02)

    exact = hit(vectors_ref, norms_ref[0:1, :])
    coarse = hit(recon_ref, norms_ref[1:2, :])
    lane = lax.broadcasted_iota(jnp.int32, (senders * count, LANES), 1)
    query = lax.broadcasted_iota(jnp.int32, (senders * count, LANES), 0)
    blocks = jnp.zeros((senders * count, LANES), jnp.float32)
    sums = jnp.zeros((1, LANES), jnp.float32)
    for k, values in enumerate((exact, coarse, exact * coarse)):
        total = jnp.sum(values, axis=1, keepdims=True)
        blocks = jnp.where(lane == k * count + query % count, total, blocks)
        sums = jnp.where(lane[:1] == 3 * count + k, jnp.sum(total, axis=0, keepdims=True), sums)
    for s in range(senders):
        row = jnp.sum(blocks[s * count : (s + 1) * count], axis=0, keepdims=True) + sums
        for p in range(out_ref.shape[0]):
            out_ref[p, s] = row


def per_device(queries, residual, codes, codebook, ranks):
    count, width = queries.shape
    rows = residual.shape[0]
    shards, copies = lax.axis_size("db"), lax.axis_size("pb")
    devices = shards * copies
    assert 3 * count + 3 <= LANES

    own_ranks = jnp.broadcast_to(ranks.astype(jnp.bfloat16)[:, None], (count, LANES))
    packed = jnp.concatenate([queries, own_ranks], axis=1)
    visiting = lax.all_to_all(
        jnp.broadcast_to(packed[None], (shards, *packed.shape)), "db", 0, 0
    )
    recon, vectors, norms = build(codes.T, jnp.transpose(codebook, (0, 2, 1)), residual)
    partial_sums = pl.pallas_call(
        count_kernel,
        out_shape=jax.ShapeDtypeStruct((copies, shards, 1, LANES), jnp.float32),
        scratch_shapes=[pltpu.VMEM((shards * count, width + LANES), jnp.float32)],
        compiler_params=pltpu.CompilerParams(vmem_limit_bytes=16 * 2**20),
        cost_estimate=pl.CostEstimate(
            flops=4 * shards * count * rows * width,
            bytes_accessed=4 * rows * width,
            transcendentals=0,
        ),
        name="count",
    )(visiting, recon, vectors, norms)
    arrived = lax.all_to_all(
        partial_sums.reshape(devices, 1, LANES), ("pb", "db"), 0, 0
    ).reshape(copies, shards, LANES)
    own = jnp.arange(copies)[:, None, None] == lax.axis_index("pb")
    hits = jnp.sum(jnp.where(own, arrived, 0.0), axis=(0, 1))[: 3 * count].reshape(3, count)
    totals = jnp.sum(arrived, axis=(0, 1))[3 * count : 3 * count + 3]
    database = rows * shards
    return hits / database, totals / (database * count * devices)


def solution(mesh):
    return jax.shard_map(
        per_device,
        mesh=mesh,
        in_specs=(P(("pb", "db"), None), P("db", None), P("db", None), P(), P(("pb", "db"))),
        out_specs=(P(None, ("pb", "db")), P()),
        check_vma=False,
    )
```

time: 216 us -> 44.8 us (0.21)
  blocking collectives: 109 us -> 0 us
  matrix products: 52.8 us -> 0 us
  local copies, waits for them, and re-layouts: 43 us -> 8.23 us
  starting transfers between devices: 0 us -> 13.3 us
  Pallas kernels: 0 us -> 13.2 us
  waiting for transfers between devices: 0 us -> 6.97 us
  other arithmetic: 6.92 us -> 2.08 us
    dot_general x19 -> x0, matrix products: 52.8 us -> none  [the longest x1 35 us: per_device(): jnp.einsum('rmc,mcj->rmj', selector, codebook, precision=lax.Precision.HI...]
    unnamed x2 -> x0, blocking collectives: 38.5 us -> none
    psum x1 -> x0, blocking collectives: 38.3 us -> none  [per_device(): totals = lax.psum(jnp.sum(hits, axis=1), ('pb', 'db')) / everyone]
    all_gather x1 -> x0, blocking collectives: 32.7 us -> none  [per_device(): lax.all_gather(queries, 'db', axis=0, tiled=True)]
    while x40 -> x0, local copies, waits for them, and re-layouts: 23.7 us -> none
    all_to_all x0 -> x2, starting transfers between devices: none -> 13.3 us  [the longest x1 7.31 us: per_device(): lax.all_to_all(jnp.broadcast_to(packed[None], (shards, *packed.shape)), '...]
    pallas_call x0 -> x2, Pallas kernels: none -> 13.2 us  [the longest x1 11.6 us: build(): pl.pallas_call(build_kernel, grid=(subspaces // group,), in_specs=[pl.Blo...]
    eq x16 -> x0, local copies, waits for them, and re-layouts: 10 us -> none  [block_hits(): code_values[:, :, None] == levels]
  transfers between devices with their start and end apart: 0 -> 2, of which waited for: 0 -> 1; matrix products, arithmetic and copies ran while one was open for 0% -> 0% of each run, Pallas kernels for 0% -> 26%
where the time goes in v1:
time: 44.8 us; the launch traced here: 44.4 us
  starting transfers between devices  13.3 us (30%)
  Pallas kernels  13.2 us (29%)
  local copies, waits for them, and re-layouts  8.23 us (18%)
  waiting for transfers between devices  6.97 us (16%)
  other arithmetic  2.08 us (5%)
  between operations  0.67 us (1%)
    pallas_call x1, Pallas kernels, build(): pl.pallas_call(build_kernel, grid=(subspaces // group,), in_specs=[pl.Blo...  11.6 us
    all_to_all x1, starting transfers between devices, per_device(): lax.all_to_all(jnp.broadcast_to(packed[None], (shards, *packed.shape)), '...  7.31 us
    all_to_all x1, waiting for transfers between devices, per_device(): lax.all_to_all(partial_sums.reshape(devices, 1, LANES), ('pb', 'db'), 0, 0)  6.97 us
    unnamed x10, local copies, waits for them, and re-layouts  6.69 us
    all_to_all x1, starting transfers between devices, per_device(): lax.all_to_all(partial_sums.reshape(devices, 1, LANES), ('pb', 'db'), 0, 0)  6.01 us
    pallas_call x1, Pallas kernels, per_device(): pl.pallas_call(count_kernel, out_shape=jax.ShapeDtypeStruct((copies, shar...  1.55 us
  transfers between devices with their start and end apart: 2, of which 1 were waited for; matrix products, arithmetic and copies ran while one was open for 0% of the time, Pallas kernels for 26%

profile of v1, /device:TPU:0, one launch (start us, length us, event | category | flops | bytes accessed | tf_op | source)
XLA Modules:
  0.0 44.4 jit_solution(1468095495303409270)
XLA Ops:
  0.6 0.7 %convert_element_type.3 = bf16[4]{0:T(256)(128)(2,1)S(1)} convert(s32[4]{0:T(128)} %param.9) | non-fusion elementwise | flops 4 | bytes 24 | tf_op jit(solution)/shard_map/convert_element_type | solution.py:119
  1.3 0.1 broadcast_in_dim.32
  1.4 0.7 %pad_maximum_fusion = bf16[4,1152]{1,0:T(4,128)(2,1)S(1)} fusion(bf16[4,128]{1,0:T(4,128)(2,1)S(1)} %broadcast_in_dim.32, bf16[4,1024]{1,0:T(4,128)(2,1)} %param.5), kind=kLoop, calls=%fused_computation.2 | loop fusion | flops 18432 | bytes 18432 | tf_op jit(solution)/shard_map/concatenate | solution.py:120
  2.1 0.6 %broadcast_in_dim.33 = bf16[8,4,1152]{2,1,0:T(4,128)(2,1)} broadcast(bf16[4,1152]{1,0:T(4,128)(2,1)S(1)} %pad_maximum_fusion), dimensions={1,2} | broadcast | bytes 82944 | tf_op jit(solution)/shard_map/broadcast_in_dim | solution.py:122
  2.7 7.3 %all-to-all-start = ((bf16[8,4,1152]{2,1,0:T(4,128)(2,1)}), bf16[8,4,1152]{2,1,0:T(4,128)(2,1)S(1)}, u32[]{:S(2)}, u32[]{:S(2)}) async-start(bf16[8,4,1152]{2,1,0:T(4,128)(2,1)} %broadcast_in_dim.33), calls=%async_computation | async-start | bytes 147456 | tf_op jit(solution)/shard_map/all_to_all | solution.py:121
  10.0 0.0 copy-start.2
  10.0 1.6 %copy-done.2 = bf16[1024,1024]{1,0:T(8,128)(2,1)S(1)} copy-done((bf16[1024,1024]{1,0:T(8,128)(2,1)S(1)}, bf16[1024,1024]{1,0:T(8,128)(2,1)}, u32[]{:S(2)}) %copy-start.2) | copy-done | bytes 2097176
  11.6 0.0 copy-start.3
  11.6 1.2 %copy-done.3 = f32[64,256,16]{1,2,0:T(8,128)S(1)} copy-done((f32[64,256,16]{1,2,0:T(8,128)S(1)}, f32[64,256,16]{1,2,0:T(8,128)}, u32[]{:S(2)}) %copy-start.3) | copy-done | bytes 1048600
  12.8 0.0 copy-start.4
  12.8 0.9 %copy-done.4 = s32[1024,64]{0,1:T(8,128)S(1)} copy-done((s32[1024,64]{0,1:T(8,128)S(1)}, s32[1024,64]{0,1:T(8,128)}, u32[]{:S(2)}) %copy-start.4) | copy-done | bytes 262168
  13.8 11.6 %build.1 = (bf16[1024,1024]{1,0:T(8,128)(2,1)S(1)}, bf16[1024,1024]{1,0:T(8,128)(2,1)S(1)}, f32[8,1024]{1,0:T(8,128)S(1)}) custom-call(s32[64,1024]{1,0:T(8,128)S(1)} %bitcast.6, f32[64,16,256]{2,1,0:T(8,128)S(1)} %bitcast.5, bf16[1024,1024]{1,0:T(8,128)(2,1)S(1)} %copy-done.2), custom_call_target="tpu_custom_call" | custom-call | flops 33554432 | bytes 8388608 | tf_op jit(solution)/shard_map/build/pallas_call | solution.py:53
  25.4 0.0 copy-start
  25.4 1.3 %copy-done = bf16[1024,1024]{1,0:T(8,128)(2,1)} copy-done((bf16[1024,1024]{1,0:T(8,128)(2,1)}, bf16[1024,1024]{1,0:T(8,128)(2,1)S(1)}, u32[]{:S(2)}) %copy-start) | copy-done | bytes 2097176
  26.7 0.0 all-to-all-done.visiting_ref
  26.7 1.6 %copy-done.1 = bf16[1024,1024]{1,0:T(8,128)(2,1)S(1)} copy-done((bf16[1024,1024]{1,0:T(8,128)(2,1)S(1)}, bf16[1024,1024]{1,0:T(8,128)(2,1)}, u32[]{:S(2)}) %copy-start.1) | copy-done | bytes 2097176
  28.3 1.6 %count.1 = f32[4,8,1,128]{3,2,1,0:T(1,128)} custom-call(bf16[8,4,1152]{2,1,0:T(4,128)(2,1)S(1)} %all-to-all-done.visiting_ref, bf16[1024,1024]{1,0:T(8,128)(2,1)S(1)} %get-tuple-element.5.recon_ref, bf16[1024,1024]{1,0:T(8,128)(2,1)S(1)} %copy-done.1, f32[8,1024]{1,0:T(8,128)S(1)} %get-tuple-element.7.norms_ref), custom_call_target="tpu_custom_call" | custom-call | flops 134217728 | bytes 4194304 | tf_op jit(solution)/shard_map/count/pallas_call | solution.py:125
  29.9 6.0 %all-to-all-start.1 = ((f32[32,1,128]{2,1,0:T(1,128)}), f32[32,1,128]{2,1,0:T(1,128)S(1)}, u32[]{:S(2)}, u32[]{:S(2)}) async-start(f32[32,1,128]{2,1,0:T(1,128)} %bitcast.3), calls=%async_computation.1 | async-start | bytes 32768 | tf_op jit(solution)/shard_map/all_to_all | solution.py:137
  35.9 0.1 broadcast_in_dim.29
  36.0 0.1 broadcast_in_dim.30
  36.1 7.0 %all-to-all-done.1 = f32[32,1,128]{2,1,0:T(1,128)S(1)} async-done(((f32[32,1,128]{2,1,0:T(1,128)}), f32[32,1,128]{2,1,0:T(1,128)S(1)}, u32[]{:S(2)}, u32[]{:S(2)}) %all-to-all-start.1) | async-done | bytes 16416 | tf_op jit(solution)/shard_map/all_to_all | solution.py:137
  43.1 0.1 fusion.1
  43.2 0.7 %div.9 = f32[3,4]{1,0:T(4,128)} reshape(f32[12]{0:T(128)S(1)} %slice_multiply_fusion.1) | data formatting | bytes 96 | tf_op jit(solution)/shard_map/div | solution.py:144
  43.8 0.6 %slice_multiply_fusion = f32[3]{0:T(128)} fusion(f32[128]{0:T(128)S(1)} %get-tuple-element.8), kind=kLoop, calls=%fused_computation.3 | loop fusion | flops 3 | bytes 24 | tf_op jit(solution)/shard_map/div | solution.py:144
  (3 shorter events, 0.0 us)
Async XLA Ops:
  2.7 24.0 %all-to-all-start = ((bf16[8,4,1152]{2,1,0:T(4,128)(2,1)}), bf16[8,4,1152]{2,1,0:T(4,128)(2,1)S(1)}, u32[]{:S(2)}, u32[]{:S(2)}) async-start(bf16[8,4,1152]{2,1,0:T(4,128)(2,1)} %broadcast_in_dim.33), calls=%async_computation | async-start | bytes 147456 | tf_op jit(solution)/shard_map/all_to_all | solution.py:121
  10.0 1.6 %copy-start.2 = (bf16[1024,1024]{1,0:T(8,128)(2,1)S(1)}, bf16[1024,1024]{1,0:T(8,128)(2,1)}, u32[]{:S(2)}) copy-start(bf16[1024,1024]{1,0:T(8,128)(2,1)} %residual_ref.1) | copy-start | bytes 6291460
  11.6 1.2 %copy-start.3 = (f32[64,256,16]{1,2,0:T(8,128)S(1)}, f32[64,256,16]{1,2,0:T(8,128)}, u32[]{:S(2)}) copy-start(f32[64,256,16]{1,2,0:T(8,128)} %param.8) | copy-start | bytes 3145732
  12.8 0.9 %copy-start.4 = (s32[1024,64]{0,1:T(8,128)S(1)}, s32[1024,64]{0,1:T(8,128)}, u32[]{:S(2)}) copy-start(s32[1024,64]{0,1:T(8,128)} %param.7) | copy-start | bytes 786436
  25.4 1.3 %copy-start = (bf16[1024,1024]{1,0:T(8,128)(2,1)}, bf16[1024,1024]{1,0:T(8,128)(2,1)S(1)}, u32[]{:S(2)}) copy-start(bf16[1024,1024]{1,0:T(8,128)(2,1)S(1)} %get-tuple-element.6.vectors_ref) | copy-start | bytes 6291460
  26.7 1.6 %copy-start.1 = (bf16[1024,1024]{1,0:T(8,128)(2,1)S(1)}, bf16[1024,1024]{1,0:T(8,128)(2,1)}, u32[]{:S(2)}) copy-start(bf16[1024,1024]{1,0:T(8,128)(2,1)} %copy-done) | copy-start | bytes 6291460
  29.9 13.2 %all-to-all-start.1 = ((f32[32,1,128]{2,1,0:T(1,128)}), f32[32,1,128]{2,1,0:T(1,128)S(1)}, u32[]{:S(2)}, u32[]{:S(2)}) async-start(f32[32,1,128]{2,1,0:T(1,128)} %bitcast.3), calls=%async_computation.1 | async-start | bytes 32768 | tf_op jit(solution)/shard_map/all_to_all | solution.py:137

commit v2 on v1

v2 whole, which is shorter than its diff:
```python
import functools

import jax
import jax.numpy as jnp
from jax import lax
from jax.experimental import pallas as pl
from jax.experimental.pallas import tpu as pltpu
from jax.sharding import PartitionSpec as P

LEVELS = 64
LANES = 128


def in_hbm(array):
    return pltpu.with_memory_space_constraint(array, pltpu.HBM)


def pack_kernel(queries_hbm, ranks_hbm, out_ref, queries, ranks, sems):
    count, width = queries.shape
    copies = (
        pltpu.make_async_copy(queries_hbm, queries, sems.at[0]),
        pltpu.make_async_copy(ranks_hbm, ranks, sems.at[1]),
    )
    for copy in copies:
        copy.start()
    for copy in copies:
        copy.wait()
    for i in range(count):
        rank = jnp.full((1, LANES), ranks[i], jnp.int32).astype(jnp.float32)
        for s in range(out_ref.shape[0]):
            out_ref[s, i : i + 1, width:] = rank.astype(jnp.bfloat16)
    for s in range(out_ref.shape[0]):
        out_ref[s, :, :width] = queries[...]


def pack(queries, ranks, receivers):
    count, width = queries.shape
    return pl.pallas_call(
        pack_kernel,
        in_specs=[pl.BlockSpec(memory_space=pltpu.HBM)] * 2,
        out_shape=jax.ShapeDtypeStruct((receivers, count, width + LANES), jnp.bfloat16),
        scratch_shapes=[
            pltpu.VMEM(queries.shape, queries.dtype),
            pltpu.SMEM(ranks.shape, ranks.dtype),
            pltpu.SemaphoreType.DMA((2,)),
        ],
        compiler_params=pltpu.CompilerParams(vmem_limit_bytes=8 * 2**20),
        name="pack",
    )(in_hbm(queries), in_hbm(ranks))


def build_kernel(
    codes_hbm, codebook_hbm, residual_hbm, values_ref, norms_ref, codes, codebook, residual, sems
):
    subspaces, subdim, centroids = codebook.shape
    rows, width = residual.shape
    group = LANES // subdim
    groups = subspaces // group
    share = lax.rem(lax.axis_index("pb"), codes_hbm.shape[1] // rows)
    own = pl.ds(pl.multiple_of(share * rows, rows), rows)

    def copies(g):
        members = pl.ds(pl.multiple_of(g * group, group), group)
        features = pl.ds(pl.multiple_of(g * LANES, LANES), LANES)
        return (
            pltpu.make_async_copy(codes_hbm.at[members, own], codes.at[g], sems.at[0, g]),
            pltpu.make_async_copy(codebook_hbm.at[members], codebook.at[members], sems.at[1, g]),
            pltpu.make_async_copy(
                residual_hbm.at[own, features], residual.at[:, features], sems.at[2, g]
            ),
        )

    for g in range(groups):
        for copy in copies(g):
            copy.start()
    norms_ref[...] = jnp.zeros_like(norms_ref)
    row = lax.broadcasted_iota(jnp.int32, (LANES, LANES), 0)
    column = lax.broadcasted_iota(jnp.int32, (LANES, LANES), 1)
    identity = (row == column).astype(jnp.bfloat16)

    def one_group(g, _):
        for copy in copies(g):
            copy.wait()
        first = pl.multiple_of(g * LANES, LANES)
        for tile in range(rows // LANES):
            at = slice(tile * LANES, (tile + 1) * LANES)
            turned = lax.dot_general(
                identity,
                residual[at, pl.ds(first, LANES)],
                (((1,), (1,)), ((), ())),
                preferred_element_type=jnp.float32,
            )
            recon_norm = jnp.zeros((subdim, LANES), jnp.float32)
            vector_norm = jnp.zeros((subdim, LANES), jnp.float32)
            for m in range(group):
                code = jnp.broadcast_to(codes[g, m : m + 1, at], (subdim, LANES))
                lane = code & (LANES - 1)
                recon = None
                for part in range(centroids // LANES):
                    table = codebook[g * group + m, :, part * LANES : (part + 1) * LANES]
                    picked = jnp.take_along_axis(table, lane, axis=1, mode="promise_in_bounds")
                    recon = picked if part == 0 else jnp.where(code >= part * LANES, picked, recon)
                vector = (recon + turned[m * subdim : (m + 1) * subdim]).astype(jnp.bfloat16)
                wide = vector.astype(jnp.float32)
                recon_norm += recon * recon
                vector_norm += wide * wide
                features = pl.ds(first + m * subdim, subdim)
                values_ref[0, features, at] = vector
                values_ref[1, features, at] = recon.astype(jnp.bfloat16)
            norms_ref[0:8, at] += sum(vector_norm[i : i + 8] for i in range(0, subdim, 8))
            norms_ref[8:16, at] += sum(recon_norm[i : i + 8] for i in range(0, subdim, 8))
        return 0

    lax.fori_loop(0, groups, one_group, 0)


def build(codes, codebook, residual, fold):
    subspaces, subdim, centroids = codebook.shape
    rows, width = residual.shape[0] // fold, residual.shape[1]
    groups = subspaces * subdim // LANES
    assert LANES % subdim == 0 and subdim % 8 == 0 and centroids % LANES == 0 and rows % LANES == 0
    return pl.pallas_call(
        build_kernel,
        in_specs=[pl.BlockSpec(memory_space=pltpu.HBM)] * 3,
        out_specs=[pl.BlockSpec(memory_space=pltpu.VMEM)] * 2,
        out_shape=[
            jax.ShapeDtypeStruct((2, width, rows), jnp.bfloat16),
            jax.ShapeDtypeStruct((16, rows), jnp.float32),
        ],
        scratch_shapes=[
            pltpu.VMEM((groups, LANES // subdim, rows), codes.dtype),
            pltpu.VMEM(codebook.shape, codebook.dtype),
            pltpu.VMEM((rows, width), residual.dtype),
            pltpu.SemaphoreType.DMA((3, groups)),
        ],
        compiler_params=pltpu.CompilerParams(vmem_limit_bytes=16 * 2**20),
        cost_estimate=pl.CostEstimate(
            flops=32 * rows * width, bytes_accessed=8 * rows * width, transcendentals=0
        ),
        name="build",
    )(in_hbm(codes), in_hbm(codebook), in_hbm(residual))


def count_kernel(visiting_ref, values_ref, norms_ref, out_ref, gathered):
    senders, count, packed = visiting_ref.shape
    width = values_ref.shape[1]
    for s in range(senders):
        gathered[s * count : (s + 1) * count, :] = visiting_ref[s].astype(jnp.float32)
    queries = gathered[:, :width]
    query_norms = jnp.sum(queries * queries, axis=1, keepdims=True)
    bounds = 1.9 + 0.6 * gathered[:, width : width + 1] / (LEVELS - 1)
    queries = queries.astype(jnp.bfloat16)

    def hit(kind):
        norms = jnp.sum(norms_ref[kind * 8 : kind * 8 + 8], axis=0, keepdims=True)
        cross = jnp.dot(queries, values_ref[kind], preferred_element_type=jnp.float32)
        distance = (query_norms + norms - 2.0 * cross) / width
        return jax.nn.sigmoid((bounds - distance) / 0.02)

    exact = hit(0)
    coarse = hit(1)
    lane = lax.broadcasted_iota(jnp.int32, (senders * count, LANES), 1)
    query = lax.broadcasted_iota(jnp.int32, (senders * count, LANES), 0)
    blocks = jnp.zeros((senders * count, LANES), jnp.float32)
    sums = jnp.zeros((1, LANES), jnp.float32)
    for k, values in enumerate((exact, coarse, exact * coarse)):
        total = jnp.sum(values, axis=1, keepdims=True)
        blocks = jnp.where(lane == k * count + query % count, total, blocks)
        sums = jnp.where(lane[:1] == 3 * count + k, jnp.sum(total, axis=0, keepdims=True), sums)
    for s in range(senders):
        row = jnp.sum(blocks[s * count : (s + 1) * count], axis=0, keepdims=True) + sums
        for p in range(out_ref.shape[0]):
            out_ref[p, s] = row


def finish_kernel(fold, database, everyone, arrived_ref, hits_ref, totals_ref):
    copies, shards = arrived_ref.shape[:2]
    count = hits_ref.shape[1]
    mine = lax.axis_index("pb") // fold
    hits = jnp.zeros((1, LANES), jnp.float32)
    totals = jnp.zeros((1, LANES), jnp.float32)
    for p in range(copies):
        arrived = jnp.sum(arrived_ref[p], axis=0)
        hits += jnp.where(mine == p // fold, arrived, 0.0)
        totals += arrived
    hits = hits / database
    totals = totals / (database * everyone)
    for k in range(3):
        hits_ref[k : k + 1, :] = hits[:, k * count : (k + 1) * count]
    totals_ref[...] = totals[:, 3 * count : 3 * count + 3]


def per_device(queries, residual, codes, codebook, ranks):
    count, width = queries.shape
    shards, copies = lax.axis_size("db"), lax.axis_size("pb")
    devices = shards * copies
    fold = 2 if copies % 2 == 0 and residual.shape[0] % (2 * LANES) == 0 else 1
    rows = residual.shape[0] // fold
    senders = fold * shards
    assert 3 * count + 3 <= LANES

    groups = [list(range(first, first + senders)) for first in range(0, devices, senders)]
    visiting = lax.all_to_all(
        pack(queries, ranks, senders), ("pb", "db"), 0, 0, axis_index_groups=groups
    )
    values, norms = build(codes.T, jnp.transpose(codebook, (0, 2, 1)), residual, fold)
    partial_sums = pl.pallas_call(
        count_kernel,
        out_shape=jax.ShapeDtypeStruct((copies // fold, senders, 1, LANES), jnp.float32),
        scratch_shapes=[pltpu.VMEM((senders * count, width + LANES), jnp.float32)],
        compiler_params=pltpu.CompilerParams(vmem_limit_bytes=16 * 2**20),
        cost_estimate=pl.CostEstimate(
            flops=4 * senders * count * rows * width,
            bytes_accessed=4 * rows * width,
            transcendentals=0,
        ),
        name="count",
    )(visiting, values, norms)
    arrived = lax.all_to_all(partial_sums.reshape(devices, 1, LANES), ("pb", "db"), 0, 0)
    hits, totals = pl.pallas_call(
        functools.partial(finish_kernel, fold, rows * senders, count * devices),
        out_shape=[
            jax.ShapeDtypeStruct((3, count), jnp.float32),
            jax.ShapeDtypeStruct((1, 3), jnp.float32),
        ],
        compiler_params=pltpu.CompilerParams(vmem_limit_bytes=8 * 2**20),
        name="finish",
    )(arrived.reshape(copies, shards, 1, LANES))
    return hits, totals[0]


def solution(mesh):
    return jax.shard_map(
        per_device,
        mesh=mesh,
        in_specs=(P(("pb", "db"), None), P("db", None), P("db", None), P(), P(("pb", "db"))),
        out_specs=(P(None, ("pb", "db")), P()),
        check_vma=False,
    )
```

time: 44.8 us -> 28.7 us (0.64)
  blocking collectives: 0 us -> 9.52 us
  local copies, waits for them, and re-layouts: 8.23 us -> 0 us
  Pallas kernels: 13.2 us -> 6.75 us
  starting transfers between devices: 13.3 us -> 7.43 us
  waiting for transfers between devices: 6.97 us -> 3.89 us
  other arithmetic: 2.08 us -> 0 us
    all_to_all x0 -> x1, blocking collectives: none -> 9.52 us  [per_device(): lax.all_to_all(partial_sums.reshape(devices, 1, LANES), ('pb', 'db'), 0, 0)]
    unnamed x10 -> x0, local copies, waits for them, and re-layouts: 6.69 us -> none
    pallas_call x2 -> x4, Pallas kernels: 13.2 us -> 6.75 us  [the longest x1 3.97 us: build(): pl.pallas_call(build_kernel, in_specs=[pl.BlockSpec(memory_space=pltpu.HB...]
    all_to_all x2 -> x1, starting transfers between devices: 13.3 us -> 7.43 us  [per_device(): lax.all_to_all(pack(queries, ranks, senders), ('pb', 'db'), 0, 0, axis_in...]
    all_to_all x2 -> x1, waiting for transfers between devices: 6.97 us -> 3.89 us  [per_device(): lax.all_to_all(pack(queries, ranks, senders), ('pb', 'db'), 0, 0, axis_in...]
    broadcast_in_dim x4 -> x0, local copies, waits for them, and re-layouts: 0.87 us -> none  [the longest x1 0.64 us: per_device(): jnp.broadcast_to(packed[None], (shards, *packed.shape))]
    concatenate x1 -> x0, other arithmetic: 0.7 us -> none  [per_device(): packed = jnp.concatenate([queries, own_ranks], axis=1)]
    div x1 -> x0, local copies, waits for them, and re-layouts: 0.67 us -> none  [per_device(): return (hits / database, totals / (database * count * devices))]
  transfers between devices with their start and end apart: 2 -> 1, of which waited for: 1 -> 1; matrix products, arithmetic and copies ran while one was open for 0% -> 0% of each run, Pallas kernels for 26% -> 14%
where the time goes in v2:
time: 28.7 us; the launch traced here: 28.2 us
  blocking collectives  9.52 us (33%)
  starting transfers between devices  7.43 us (26%)
  Pallas kernels  6.75 us (24%)
  waiting for transfers between devices  3.89 us (14%)
  between operations  0.66 us (2%)
    all_to_all x1, blocking collectives, per_device(): lax.all_to_all(partial_sums.reshape(devices, 1, LANES), ('pb', 'db'), 0, 0)  9.52 us
    all_to_all x1, starting transfers between devices, per_device(): lax.all_to_all(pack(queries, ranks, senders), ('pb', 'db'), 0, 0, axis_in...  7.43 us
    pallas_call x1, Pallas kernels, build(): pl.pallas_call(build_kernel, in_specs=[pl.BlockSpec(memory_space=pltpu.HB...  3.97 us
    all_to_all x1, waiting for transfers between devices, per_device(): lax.all_to_all(pack(queries, ranks, senders), ('pb', 'db'), 0, 0, axis_in...  3.89 us
    pallas_call x1, Pallas kernels, pack(): pl.pallas_call(pack_kernel, in_specs=[pl.BlockSpec(memory_space=pltpu.HBM...  1.5 us
    pallas_call x1, Pallas kernels, per_device(): pl.pallas_call(functools.partial(finish_kernel, fold, rows * senders, cou...  0.67 us
    pallas_call x1, Pallas kernels, per_device(): pl.pallas_call(count_kernel, out_shape=jax.ShapeDtypeStruct((copies // fo...  0.61 us
  transfers between devices with their start and end apart: 1, of which 1 were waited for; matrix products, arithmetic and copies ran while one was open for 0% of the time, Pallas kernels for 14%

profile of v2, /device:TPU:0, one launch (start us, length us, event | category | flops | bytes accessed | tf_op | source)
XLA Modules:
  0.0 28.2 jit_solution(11941164843189588746)
XLA Ops:
  0.6 1.5 %pack.1 = bf16[16,4,1152]{2,1,0:T(4,128)(2,1)} custom-call(bf16[4,1024]{1,0:T(4,128)(2,1)} %queries_hbm.1, s32[4]{0:T(128)} %ranks_hbm.1), custom_call_target="tpu_custom_call" | custom-call | tf_op jit(solution)/shard_map/pack/pallas_call | solution.py:38
  2.1 7.4 %all-to-all-start = ((bf16[16,4,1152]{2,1,0:T(4,128)(2,1)}), bf16[16,4,1152]{2,1,0:T(4,128)(2,1)S(1)}, u32[]{:S(2)}, u32[]{:S(2)}) async-start(bf16[16,4,1152]{2,1,0:T(4,128)(2,1)} %pack.1), calls=%async_computation | async-start | bytes 294912 | tf_op jit(solution)/shard_map/all_to_all | solution.py:203
  9.6 4.0 %build.1 = (bf16[2,1024,512]{2,1,0:T(8,128)(2,1)S(1)}, f32[16,512]{1,0:T(8,128)S(1)}) custom-call(s32[64,1024]{1,0:T(8,128)} %bitcast.10, f32[64,16,256]{2,1,0:T(8,128)} %bitcast.9, bf16[1024,1024]{1,0:T(8,128)(2,1)} %residual_hbm.1), custom_call_target="tpu_custom_call" | custom-call | flops 16777216 | bytes 4194304 | tf_op jit(solution)/shard_map/build/pallas_call | solution.py:122
  13.6 3.9 %all-to-all-done.visiting_ref = bf16[16,4,1152]{2,1,0:T(4,128)(2,1)S(1)} async-done(((bf16[16,4,1152]{2,1,0:T(4,128)(2,1)}), bf16[16,4,1152]{2,1,0:T(4,128)(2,1)S(1)}, u32[]{:S(2)}, u32[]{:S(2)}) %all-to-all-start) | async-done | bytes 147488 | tf_op jit(solution)/shard_map/all_to_all | solution.py:203
  17.4 0.6 %count.1 = f32[2,16,1,128]{3,2,1,0:T(1,128)S(1)} custom-call(bf16[16,4,1152]{2,1,0:T(4,128)(2,1)S(1)} %all-to-all-done.visiting_ref, bf16[2,1024,512]{2,1,0:T(8,128)(2,1)S(1)} %get-tuple-element.6.values_ref, f32[16,512]{1,0:T(8,128)S(1)} %get-tuple-element.7.norms_ref), custom_call_target="tpu_custom_call" | custom-call | flops 134217728 | bytes 2097152 | tf_op jit(solution)/shard_map/count/pallas_call | solution.py:207
  18.1 9.5 %all_to_all.10 = f32[32,1,128]{2,1,0:T(1,128)S(1)} all-to-all(f32[32,1,128]{2,1,0:T(1,128)S(1)} %bitcast.7), channel_id=1, replica_groups=mesh['pb'=4,'db'=8] {'pb','db'}, dimensions={0} | all-to-all | bytes 32768 | tf_op jit(solution)/shard_map/all_to_all | solution.py:219
  27.6 0.7 %finish.1 = (f32[3,4]{1,0:T(4,128)}, f32[1,3]{1,0:T(1,128)}) custom-call(f32[4,8,1,128]{3,2,1,0:T(1,128)S(1)} %bitcast.8), custom_call_target="tpu_custom_call" | custom-call | tf_op jit(solution)/shard_map/finish/pallas_call | solution.py:220
Async XLA Ops:
  2.1 15.3 %all-to-all-start = ((bf16[16,4,1152]{2,1,0:T(4,128)(2,1)}), bf16[16,4,1152]{2,1,0:T(4,128)(2,1)S(1)}, u32[]{:S(2)}, u32[]{:S(2)}) async-start(bf16[16,4,1152]{2,1,0:T(4,128)(2,1)} %pack.1), calls=%async_computation | async-start | bytes 294912 | tf_op jit(solution)/shard_map/all_to_all | solution.py:203

commit v3 on v2

--- a/solution.py
+++ b/solution.py
@@ -141,7 +141,7 @@
     )(in_hbm(codes), in_hbm(codebook), in_hbm(residual))
 
 
-def count_kernel(visiting_ref, values_ref, norms_ref, out_ref, gathered):
+def count_kernel(order, visiting_ref, values_ref, norms_ref, out_ref, gathered):
     senders, count, packed = visiting_ref.shape
     width = values_ref.shape[1]
     for s in range(senders):
@@ -170,7 +170,7 @@
     for s in range(senders):
         row = jnp.sum(blocks[s * count : (s + 1) * count], axis=0, keepdims=True) + sums
         for p in range(out_ref.shape[0]):
-            out_ref[p, s] = row
+            out_ref[p, order[s]] = row
 
 
 def finish_kernel(fold, database, everyone, arrived_ref, hits_ref, totals_ref):
@@ -199,13 +199,15 @@
     senders = fold * shards
     assert 3 * count + 3 <= LANES
 
-    groups = [list(range(first, first + senders)) for first in range(0, devices, senders)]
+    order = list(range(senders))
+    order.insert(0, order.pop(senders - shards // 2))
+    groups = [[first + at for at in order] for first in range(0, devices, senders)]
     visiting = lax.all_to_all(
         pack(queries, ranks, senders), ("pb", "db"), 0, 0, axis_index_groups=groups
     )
     values, norms = build(codes.T, jnp.transpose(codebook, (0, 2, 1)), residual, fold)
     partial_sums = pl.pallas_call(
-        count_kernel,
+        functools.partial(count_kernel, order),
         out_shape=jax.ShapeDtypeStruct((copies // fold, senders, 1, LANES), jnp.float32),
         scratch_shapes=[pltpu.VMEM((senders * count, width + LANES), jnp.float32)],
         compiler_params=pltpu.CompilerParams(vmem_limit_bytes=16 * 2**20),

time: 28.7 us -> 27.6 us (0.962)
  waiting for transfers between devices: 3.89 us -> 1.64 us
  blocking collectives: 9.52 us -> 10.5 us
    all_to_all x1, waiting for transfers between devices: 3.89 us -> 1.64 us  [per_device(): lax.all_to_all(pack(queries, ranks, senders), ('pb', 'db'), 0, 0, axis_in...]
    all_to_all x1, blocking collectives: 9.52 us -> 10.5 us  [per_device(): lax.all_to_all(partial_sums.reshape(devices, 1, LANES), ('pb', 'db'), 0, 0)]
  transfers between devices with their start and end apart: 1 -> 1, of which waited for: 1 -> 1; matrix products, arithmetic and copies ran while one was open for 0% -> 0% of each run, Pallas kernels for 14% -> 15%
where the time goes in v3:
time: 27.6 us; the launch traced here: 27.2 us
  blocking collectives  10.5 us (38%)
  starting transfers between devices  7.62 us (28%)
  Pallas kernels  6.75 us (24%)
  waiting for transfers between devices  1.64 us (6%)
  between operations  0.65 us (2%)
    all_to_all x1, blocking collectives, per_device(): lax.all_to_all(partial_sums.reshape(devices, 1, LANES), ('pb', 'db'), 0, 0)  10.5 us
    all_to_all x1, starting transfers between devices, per_device(): lax.all_to_all(pack(queries, ranks, senders), ('pb', 'db'), 0, 0, axis_in...  7.62 us
    pallas_call x1, Pallas kernels, build(): pl.pallas_call(build_kernel, in_specs=[pl.BlockSpec(memory_space=pltpu.HB...  3.96 us
    all_to_all x1, waiting for transfers between devices, per_device(): lax.all_to_all(pack(queries, ranks, senders), ('pb', 'db'), 0, 0, axis_in...  1.64 us
    pallas_call x1, Pallas kernels, pack(): pl.pallas_call(pack_kernel, in_specs=[pl.BlockSpec(memory_space=pltpu.HBM...  1.5 us
    pallas_call x1, Pallas kernels, per_device(): pl.pallas_call(functools.partial(finish_kernel, fold, rows * senders, cou...  0.67 us
    pallas_call x1, Pallas kernels, per_device(): pl.pallas_call(functools.partial(count_kernel, order), out_shape=jax.Shap...  0.61 us
  transfers between devices with their start and end apart: 1, of which 1 were waited for; matrix products, arithmetic and copies ran while one was open for 0% of the time, Pallas kernels for 15%

profile of v3, /device:TPU:0, one launch (start us, length us, event | category | flops | bytes accessed | tf_op | source)
XLA Modules:
  0.0 27.2 jit_solution(17788910587581741645)
XLA Ops:
  0.6 1.5 %pack.1 = bf16[16,4,1152]{2,1,0:T(4,128)(2,1)} custom-call(bf16[4,1024]{1,0:T(4,128)(2,1)} %queries_hbm.1, s32[4]{0:T(128)} %ranks_hbm.1), custom_call_target="tpu_custom_call" | custom-call | tf_op jit(solution)/shard_map/pack/pallas_call | solution.py:38
  2.1 7.6 %all-to-all-start = ((bf16[16,4,1152]{2,1,0:T(4,128)(2,1)}), bf16[16,4,1152]{2,1,0:T(4,128)(2,1)S(1)}, u32[]{:S(2)}, u32[]{:S(2)}) async-start(bf16[16,4,1152]{2,1,0:T(4,128)(2,1)} %pack.1), calls=%async_computation | async-start | bytes 294912 | tf_op jit(solution)/shard_map/all_to_all | solution.py:205
  9.8 4.0 %build.1 = (bf16[2,1024,512]{2,1,0:T(8,128)(2,1)S(1)}, f32[16,512]{1,0:T(8,128)S(1)}) custom-call(s32[64,1024]{1,0:T(8,128)} %bitcast.10, f32[64,16,256]{2,1,0:T(8,128)} %bitcast.9, bf16[1024,1024]{1,0:T(8,128)(2,1)} %residual_hbm.1), custom_call_target="tpu_custom_call" | custom-call | flops 16777216 | bytes 4194304 | tf_op jit(solution)/shard_map/build/pallas_call | solution.py:122
  13.7 1.6 %all-to-all-done.visiting_ref = bf16[16,4,1152]{2,1,0:T(4,128)(2,1)S(1)} async-done(((bf16[16,4,1152]{2,1,0:T(4,128)(2,1)}), bf16[16,4,1152]{2,1,0:T(4,128)(2,1)S(1)}, u32[]{:S(2)}, u32[]{:S(2)}) %all-to-all-start) | async-done | bytes 147488 | tf_op jit(solution)/shard_map/all_to_all | solution.py:205
  15.4 0.6 %count.1 = f32[2,16,1,128]{3,2,1,0:T(1,128)S(1)} custom-call(bf16[16,4,1152]{2,1,0:T(4,128)(2,1)S(1)} %all-to-all-done.visiting_ref, bf16[2,1024,512]{2,1,0:T(8,128)(2,1)S(1)} %get-tuple-element.6.values_ref, f32[16,512]{1,0:T(8,128)S(1)} %get-tuple-element.7.norms_ref), custom_call_target="tpu_custom_call" | custom-call | flops 134217728 | bytes 2097152 | tf_op jit(solution)/shard_map/count/pallas_call | solution.py:209
  16.0 10.5 %all_to_all.10 = f32[32,1,128]{2,1,0:T(1,128)S(1)} all-to-all(f32[32,1,128]{2,1,0:T(1,128)S(1)} %bitcast.7), channel_id=1, replica_groups=mesh['pb'=4,'db'=8] {'pb','db'}, dimensions={0} | all-to-all | bytes 32768 | tf_op jit(solution)/shard_map/all_to_all | solution.py:221
  26.5 0.7 %finish.1 = (f32[3,4]{1,0:T(4,128)}, f32[1,3]{1,0:T(1,128)}) custom-call(f32[4,8,1,128]{3,2,1,0:T(1,128)S(1)} %bitcast.8), custom_call_target="tpu_custom_call" | custom-call | tf_op jit(solution)/shard_map/finish/pallas_call | solution.py:222
Async XLA Ops:
  2.1 13.2 %all-to-all-start = ((bf16[16,4,1152]{2,1,0:T(4,128)(2,1)}), bf16[16,4,1152]{2,1,0:T(4,128)(2,1)S(1)}, u32[]{:S(2)}, u32[]{:S(2)}) async-start(bf16[16,4,1152]{2,1,0:T(4,128)(2,1)} %pack.1), calls=%async_computation | async-start | bytes 294912 | tf_op jit(solution)/shard_map/all_to_all | solution.py:205

commit v4 on v3

--- a/solution.py
+++ b/solution.py
@@ -18,8 +18,8 @@
 def pack_kernel(queries_hbm, ranks_hbm, out_ref, queries, ranks, sems):
     count, width = queries.shape
     copies = (
+        pltpu.make_async_copy(ranks_hbm, ranks, sems.at[1]),
         pltpu.make_async_copy(queries_hbm, queries, sems.at[0]),
-        pltpu.make_async_copy(ranks_hbm, ranks, sems.at[1]),
     )
     for copy in copies:
         copy.start()
@@ -101,12 +101,12 @@
                     picked = jnp.take_along_axis(table, lane, axis=1, mode="promise_in_bounds")
                     recon = picked if part == 0 else jnp.where(code >= part * LANES, picked, recon)
                 vector = (recon + turned[m * subdim : (m + 1) * subdim]).astype(jnp.bfloat16)
-                wide = vector.astype(jnp.float32)
-                recon_norm += recon * recon
-                vector_norm += wide * wide
+                rounded = recon.astype(jnp.bfloat16)
+                recon_norm += rounded.astype(jnp.float32) ** 2
+                vector_norm += vector.astype(jnp.float32) ** 2
                 features = pl.ds(first + m * subdim, subdim)
                 values_ref[0, features, at] = vector
-                values_ref[1, features, at] = recon.astype(jnp.bfloat16)
+                values_ref[1, features, at] = rounded
             norms_ref[0:8, at] += sum(vector_norm[i : i + 8] for i in range(0, subdim, 8))
             norms_ref[8:16, at] += sum(recon_norm[i : i + 8] for i in range(0, subdim, 8))
         return 0

time: 27.6 us -> 27.5 us (level)
  no operation moved by 1% of the time
where the time goes in v4:
time: 27.5 us; the launch traced here: 27.1 us
  blocking collectives  10.5 us (38%)
  starting transfers between devices  7.62 us (28%)
  Pallas kernels  6.64 us (24%)
  waiting for transfers between devices  1.64 us (6%)
  between operations  0.65 us (2%)
    all_to_all x1, blocking collectives, per_device(): lax.all_to_all(partial_sums.reshape(devices, 1, LANES), ('pb', 'db'), 0, 0)  10.5 us
    all_to_all x1, starting transfers between devices, per_device(): lax.all_to_all(pack(queries, ranks, senders), ('pb', 'db'), 0, 0, axis_in...  7.62 us
    pallas_call x1, Pallas kernels, build(): pl.pallas_call(build_kernel, in_specs=[pl.BlockSpec(memory_space=pltpu.HB...  3.96 us
    all_to_all x1, waiting for transfers between devices, per_device(): lax.all_to_all(pack(queries, ranks, senders), ('pb', 'db'), 0, 0, axis_in...  1.64 us
    pallas_call x1, Pallas kernels, pack(): pl.pallas_call(pack_kernel, in_specs=[pl.BlockSpec(memory_space=pltpu.HBM...  1.41 us
    pallas_call x1, Pallas kernels, per_device(): pl.pallas_call(functools.partial(finish_kernel, fold, rows * senders, cou...  0.67 us
    pallas_call x1, Pallas kernels, per_device(): pl.pallas_call(functools.partial(count_kernel, order), out_shape=jax.Shap...  0.6 us
  transfers between devices with their start and end apart: 1, of which 1 were waited for; matrix products, arithmetic and copies ran while one was open for 0% of the time, Pallas kernels for 15%

profile of v4, /device:TPU:0, one launch (start us, length us, event | category | flops | bytes accessed | tf_op | source)
XLA Modules:
  0.0 27.1 jit_solution(16371127945482262260)
XLA Ops:
  0.6 1.4 %pack.1 = bf16[16,4,1152]{2,1,0:T(4,128)(2,1)} custom-call(bf16[4,1024]{1,0:T(4,128)(2,1)} %queries_hbm.1, s32[4]{0:T(128)} %ranks_hbm.1), custom_call_target="tpu_custom_call" | custom-call | tf_op jit(solution)/shard_map/pack/pallas_call | solution.py:38
  2.0 7.6 %all-to-all-start = ((bf16[16,4,1152]{2,1,0:T(4,128)(2,1)}), bf16[16,4,1152]{2,1,0:T(4,128)(2,1)S(1)}, u32[]{:S(2)}, u32[]{:S(2)}) async-start(bf16[16,4,1152]{2,1,0:T(4,128)(2,1)} %pack.1), calls=%async_computation | async-start | bytes 294912 | tf_op jit(solution)/shard_map/all_to_all | solution.py:205
  9.7 4.0 %build.1 = (bf16[2,1024,512]{2,1,0:T(8,128)(2,1)S(1)}, f32[16,512]{1,0:T(8,128)S(1)}) custom-call(s32[64,1024]{1,0:T(8,128)} %bitcast.10, f32[64,16,256]{2,1,0:T(8,128)} %bitcast.9, bf16[1024,1024]{1,0:T(8,128)(2,1)} %residual_hbm.1), custom_call_target="tpu_custom_call" | custom-call | flops 16777216 | bytes 4194304 | tf_op jit(solution)/shard_map/build/pallas_call | solution.py:122
  13.6 1.6 %all-to-all-done.visiting_ref = bf16[16,4,1152]{2,1,0:T(4,128)(2,1)S(1)} async-done(((bf16[16,4,1152]{2,1,0:T(4,128)(2,1)}), bf16[16,4,1152]{2,1,0:T(4,128)(2,1)S(1)}, u32[]{:S(2)}, u32[]{:S(2)}) %all-to-all-start) | async-done | bytes 147488 | tf_op jit(solution)/shard_map/all_to_all | solution.py:205
  15.3 0.6 %count.1 = f32[2,16,1,128]{3,2,1,0:T(1,128)S(1)} custom-call(bf16[16,4,1152]{2,1,0:T(4,128)(2,1)S(1)} %all-to-all-done.visiting_ref, bf16[2,1024,512]{2,1,0:T(8,128)(2,1)S(1)} %get-tuple-element.6.values_ref, f32[16,512]{1,0:T(8,128)S(1)} %get-tuple-element.7.norms_ref), custom_call_target="tpu_custom_call" | custom-call | flops 134217728 | bytes 2097152 | tf_op jit(solution)/shard_map/count/pallas_call | solution.py:209
  15.9 10.5 %all_to_all.10 = f32[32,1,128]{2,1,0:T(1,128)S(1)} all-to-all(f32[32,1,128]{2,1,0:T(1,128)S(1)} %bitcast.7), channel_id=1, replica_groups=mesh['pb'=4,'db'=8] {'pb','db'}, dimensions={0} | all-to-all | bytes 32768 | tf_op jit(solution)/shard_map/all_to_all | solution.py:221
  26.4 0.7 %finish.1 = (f32[3,4]{1,0:T(4,128)}, f32[1,3]{1,0:T(1,128)}) custom-call(f32[4,8,1,128]{3,2,1,0:T(1,128)S(1)} %bitcast.8), custom_call_target="tpu_custom_call" | custom-call | tf_op jit(solution)/shard_map/finish/pallas_call | solution.py:222
Async XLA Ops:
  2.0 13.2 %all-to-all-start = ((bf16[16,4,1152]{2,1,0:T(4,128)(2,1)}), bf16[16,4,1152]{2,1,0:T(4,128)(2,1)S(1)}, u32[]{:S(2)}, u32[]{:S(2)}) async-start(bf16[16,4,1152]{2,1,0:T(4,128)(2,1)} %pack.1), calls=%async_computation | async-start | bytes 294912 | tf_op jit(solution)/shard_map/all_to_all | solution.py:205

commit v5 on v4

--- a/solution.py
+++ b/solution.py
@@ -1,4 +1,5 @@
 import functools
+import math
 
 import jax
 import jax.numpy as jnp
@@ -199,8 +200,8 @@
     senders = fold * shards
     assert 3 * count + 3 <= LANES
 
-    order = list(range(senders))
-    order.insert(0, order.pop(senders - shards // 2))
+    stride = senders // 2 - 1 if math.gcd(senders // 2 - 1, senders) == 1 else 1
+    order = [(senders - shards // 2 - 1 + stride * i) % senders for i in range(senders)]
     groups = [[first + at for at in order] for first in range(0, devices, senders)]
     visiting = lax.all_to_all(
         pack(queries, ranks, senders), ("pb", "db"), 0, 0, axis_index_groups=groups

time: 27.5 us -> 27.2 us (0.989)
  blocking collectives: 10.5 us -> 10.1 us
    all_to_all x1, blocking collectives: 10.5 us -> 10.1 us  [per_device(): lax.all_to_all(partial_sums.reshape(devices, 1, LANES), ('pb', 'db'), 0, 0)]
where the time goes in v5:
time: 27.2 us; the launch traced here: 26.8 us
  blocking collectives  10.1 us (37%)
  starting transfers between devices  7.62 us (28%)
  Pallas kernels  6.64 us (24%)
  waiting for transfers between devices  1.84 us (7%)
  between operations  0.65 us (2%)
    all_to_all x1, blocking collectives, per_device(): lax.all_to_all(partial_sums.reshape(devices, 1, LANES), ('pb', 'db'), 0, 0)  10.1 us
    all_to_all x1, starting transfers between devices, per_device(): lax.all_to_all(pack(queries, ranks, senders), ('pb', 'db'), 0, 0, axis_in...  7.62 us
    pallas_call x1, Pallas kernels, build(): pl.pallas_call(build_kernel, in_specs=[pl.BlockSpec(memory_space=pltpu.HB...  3.96 us
    all_to_all x1, waiting for transfers between devices, per_device(): lax.all_to_all(pack(queries, ranks, senders), ('pb', 'db'), 0, 0, axis_in...  1.84 us
    pallas_call x1, Pallas kernels, pack(): pl.pallas_call(pack_kernel, in_specs=[pl.BlockSpec(memory_space=pltpu.HBM...  1.41 us
    pallas_call x1, Pallas kernels, per_device(): pl.pallas_call(functools.partial(finish_kernel, fold, rows * senders, cou...  0.67 us
    pallas_call x1, Pallas kernels, per_device(): pl.pallas_call(functools.partial(count_kernel, order), out_shape=jax.Shap...  0.61 us
  transfers between devices with their start and end apart: 1, of which 1 were waited for; matrix products, arithmetic and copies ran while one was open for 0% of the time, Pallas kernels for 15%

profile of v5, /device:TPU:0, one launch (start us, length us, event | category | flops | bytes accessed | tf_op | source)
XLA Modules:
  0.0 26.8 jit_solution(5544167406364167000)
XLA Ops:
  0.6 1.4 %pack.1 = bf16[16,4,1152]{2,1,0:T(4,128)(2,1)} custom-call(bf16[4,1024]{1,0:T(4,128)(2,1)} %queries_hbm.1, s32[4]{0:T(128)} %ranks_hbm.1), custom_call_target="tpu_custom_call" | custom-call | tf_op jit(solution)/shard_map/pack/pallas_call | solution.py:39
  2.0 7.6 %all-to-all-start = ((bf16[16,4,1152]{2,1,0:T(4,128)(2,1)}), bf16[16,4,1152]{2,1,0:T(4,128)(2,1)S(1)}, u32[]{:S(2)}, u32[]{:S(2)}) async-start(bf16[16,4,1152]{2,1,0:T(4,128)(2,1)} %pack.1), calls=%async_computation | async-start | bytes 294912 | tf_op jit(solution)/shard_map/all_to_all | solution.py:206
  9.7 4.0 %build.1 = (bf16[2,1024,512]{2,1,0:T(8,128)(2,1)S(1)}, f32[16,512]{1,0:T(8,128)S(1)}) custom-call(s32[64,1024]{1,0:T(8,128)} %bitcast.10, f32[64,16,256]{2,1,0:T(8,128)} %bitcast.9, bf16[1024,1024]{1,0:T(8,128)(2,1)} %residual_hbm.1), custom_call_target="tpu_custom_call" | custom-call | flops 16777216 | bytes 4194304 | tf_op jit(solution)/shard_map/build/pallas_call | solution.py:123
  13.6 1.8 %all-to-all-done.visiting_ref = bf16[16,4,1152]{2,1,0:T(4,128)(2,1)S(1)} async-done(((bf16[16,4,1152]{2,1,0:T(4,128)(2,1)}), bf16[16,4,1152]{2,1,0:T(4,128)(2,1)S(1)}, u32[]{:S(2)}, u32[]{:S(2)}) %all-to-all-start) | async-done | bytes 147488 | tf_op jit(solution)/shard_map/all_to_all | solution.py:206
  15.5 0.6 %count.1 = f32[2,16,1,128]{3,2,1,0:T(1,128)S(1)} custom-call(bf16[16,4,1152]{2,1,0:T(4,128)(2,1)S(1)} %all-to-all-done.visiting_ref, bf16[2,1024,512]{2,1,0:T(8,128)(2,1)S(1)} %get-tuple-element.6.values_ref, f32[16,512]{1,0:T(8,128)S(1)} %get-tuple-element.7.norms_ref), custom_call_target="tpu_custom_call" | custom-call | flops 134217728 | bytes 2097152 | tf_op jit(solution)/shard_map/count/pallas_call | solution.py:210
  16.1 10.1 %all_to_all.10 = f32[32,1,128]{2,1,0:T(1,128)S(1)} all-to-all(f32[32,1,128]{2,1,0:T(1,128)S(1)} %bitcast.7), channel_id=1, replica_groups=mesh['pb'=4,'db'=8] {'pb','db'}, dimensions={0} | all-to-all | bytes 32768 | tf_op jit(solution)/shard_map/all_to_all | solution.py:222
  26.2 0.7 %finish.1 = (f32[3,4]{1,0:T(4,128)}, f32[1,3]{1,0:T(1,128)}) custom-call(f32[4,8,1,128]{3,2,1,0:T(1,128)S(1)} %bitcast.8), custom_call_target="tpu_custom_call" | custom-call | tf_op jit(solution)/shard_map/finish/pallas_call | solution.py:223
Async XLA Ops:
  2.0 13.4 %all-to-all-start = ((bf16[16,4,1152]{2,1,0:T(4,128)(2,1)}), bf16[16,4,1152]{2,1,0:T(4,128)(2,1)S(1)}, u32[]{:S(2)}, u32[]{:S(2)}) async-start(bf16[16,4,1152]{2,1,0:T(4,128)(2,1)} %pack.1), calls=%async_computation | async-start | bytes 294912 | tf_op jit(solution)/shard_map/all_to_all | solution.py:206

commit v6 on v5

--- a/solution.py
+++ b/solution.py
@@ -26,20 +26,28 @@
         copy.start()
     for copy in copies:
         copy.wait()
+    receivers, lines, _ = out_ref.shape
+    line = lax.broadcasted_iota(jnp.int32, (lines, LANES), 0)
+    lane = lax.broadcasted_iota(jnp.int32, (lines, LANES), 1)
+    rank = jnp.zeros((lines, LANES), jnp.int32)
     for i in range(count):
-        rank = jnp.full((1, LANES), ranks[i], jnp.int32).astype(jnp.float32)
-        for s in range(out_ref.shape[0]):
-            out_ref[s, i : i + 1, width:] = rank.astype(jnp.bfloat16)
-    for s in range(out_ref.shape[0]):
-        out_ref[s, :, :width] = queries[...]
-
-
-def pack(queries, ranks, receivers):
+        rank = jnp.where((line == i % lines) & (lane == i // lines), ranks[i], rank)
+    rank = rank.astype(jnp.float32).astype(jnp.bfloat16)
+    parts = [queries[i * lines : (i + 1) * lines, :] for i in range(count // lines)]
+    for s in range(receivers):
+        for i, part in enumerate(parts):
+            out_ref[s, :, i * width : (i + 1) * width] = part
+        out_ref[s, :, len(parts) * width :] = rank
+
+
+def pack(queries, ranks, receivers, lines):
     count, width = queries.shape
     return pl.pallas_call(
         pack_kernel,
         in_specs=[pl.BlockSpec(memory_space=pltpu.HBM)] * 2,
-        out_shape=jax.ShapeDtypeStruct((receivers, count, width + LANES), jnp.bfloat16),
+        out_shape=jax.ShapeDtypeStruct(
+            (receivers, lines, count // lines * width + LANES), jnp.bfloat16
+        ),
         scratch_shapes=[
             pltpu.VMEM(queries.shape, queries.dtype),
             pltpu.SMEM(ranks.shape, ranks.dtype),
@@ -143,10 +151,17 @@
 
 
 def count_kernel(order, visiting_ref, values_ref, norms_ref, out_ref, gathered):
-    senders, count, packed = visiting_ref.shape
+    senders, lines, _ = visiting_ref.shape
     width = values_ref.shape[1]
+    parts = gathered.shape[0] // (senders * lines)
+    count = parts * lines
     for s in range(senders):
-        gathered[s * count : (s + 1) * count, :] = visiting_ref[s].astype(jnp.float32)
+        tail = visiting_ref[s, :, parts * width :].astype(jnp.float32)
+        for i in range(parts):
+            rows = slice((i * senders + s) * lines, (i * senders + s + 1) * lines)
+            part = visiting_ref[s, :, i * width : (i + 1) * width]
+            gathered[rows, :width] = part.astype(jnp.float32)
+            gathered[rows, width:] = jnp.broadcast_to(tail[:, i : i + 1], (lines, LANES))
     queries = gathered[:, :width]
     query_norms = jnp.sum(queries * queries, axis=1, keepdims=True)
     bounds = 1.9 + 0.6 * gathered[:, width : width + 1] / (LEVELS - 1)
@@ -166,10 +181,14 @@
     sums = jnp.zeros((1, LANES), jnp.float32)
     for k, values in enumerate((exact, coarse, exact * coarse)):
         total = jnp.sum(values, axis=1, keepdims=True)
-        blocks = jnp.where(lane == k * count + query % count, total, blocks)
+        mine = query // (senders * lines) * lines + query % lines
+        blocks = jnp.where(lane == k * count + mine, total, blocks)
         sums = jnp.where(lane[:1] == 3 * count + k, jnp.sum(total, axis=0, keepdims=True), sums)
     for s in range(senders):
-        row = jnp.sum(blocks[s * count : (s + 1) * count], axis=0, keepdims=True) + sums
+        row = sums
+        for i in range(parts):
+            first = (i * senders + s) * lines
+            row += jnp.sum(blocks[first : first + lines], axis=0, keepdims=True)
         for p in range(out_ref.shape[0]):
             out_ref[p, order[s]] = row
 
@@ -198,13 +217,14 @@
     fold = 2 if copies % 2 == 0 and residual.shape[0] % (2 * LANES) == 0 else 1
     rows = residual.shape[0] // fold
     senders = fold * shards
+    lines = 2 if count % 2 == 0 else count
     assert 3 * count + 3 <= LANES
 
     stride = senders // 2 - 1 if math.gcd(senders // 2 - 1, senders) == 1 else 1
     order = [(senders - shards // 2 - 1 + stride * i) % senders for i in range(senders)]
     groups = [[first + at for at in order] for first in range(0, devices, senders)]
     visiting = lax.all_to_all(
-        pack(queries, ranks, senders), ("pb", "db"), 0, 0, axis_index_groups=groups
+        pack(queries, ranks, senders, lines), ("pb", "db"), 0, 0, axis_index_groups=groups
     )
     values, norms = build(codes.T, jnp.transpose(codebook, (0, 2, 1)), residual, fold)
     partial_sums = pl.pallas_call(

time: 27.2 us -> 27.2 us (level)
  no operation moved by 1% of the time
where the time goes in v6:
time: 27.2 us; the launch traced here: 26.8 us
  blocking collectives  10.1 us (37%)
  starting transfers between devices  7.62 us (28%)
  Pallas kernels  6.64 us (24%)
  waiting for transfers between devices  1.71 us (6%)
  between operations  0.65 us (2%)
    all_to_all x1, blocking collectives, per_device(): lax.all_to_all(partial_sums.reshape(devices, 1, LANES), ('pb', 'db'), 0, 0)  10.1 us
    all_to_all x1, starting transfers between devices, per_device(): lax.all_to_all(pack(queries, ranks, senders, lines), ('pb', 'db'), 0, 0,...  7.62 us
    pallas_call x1, Pallas kernels, build(): pl.pallas_call(build_kernel, in_specs=[pl.BlockSpec(memory_space=pltpu.HB...  3.96 us
    all_to_all x1, waiting for transfers between devices, per_device(): lax.all_to_all(pack(queries, ranks, senders, lines), ('pb', 'db'), 0, 0,...  1.71 us
    pallas_call x1, Pallas kernels, pack(): pl.pallas_call(pack_kernel, in_specs=[pl.BlockSpec(memory_space=pltpu.HBM...  1.37 us
    pallas_call x1, Pallas kernels, per_device(): pl.pallas_call(functools.partial(finish_kernel, fold, rows * senders, cou...  0.67 us
    pallas_call x1, Pallas kernels, per_device(): pl.pallas_call(functools.partial(count_kernel, order), out_shape=jax.Shap...  0.64 us
  transfers between devices with their start and end apart: 1, of which 1 were waited for; matrix products, arithmetic and copies ran while one was open for 0% of the time, Pallas kernels for 15%

profile of v6, /device:TPU:0, one launch (start us, length us, event | category | flops | bytes accessed | tf_op | source)
XLA Modules:
  0.0 26.8 jit_solution(1067368014225179008)
XLA Ops:
  0.6 1.4 %pack.1 = bf16[16,2,2176]{2,1,0:T(2,128)(2,1)} custom-call(bf16[4,1024]{1,0:T(4,128)(2,1)} %queries_hbm.1, s32[4]{0:T(128)} %ranks_hbm.1), custom_call_target="tpu_custom_call" | custom-call | tf_op jit(solution)/shard_map/pack/pallas_call | solution.py:45
  2.0 7.6 %all-to-all-start = ((bf16[16,2,2176]{2,1,0:T(2,128)(2,1)}), bf16[16,2,2176]{2,1,0:T(2,128)(2,1)S(1)}, u32[]{:S(2)}, u32[]{:S(2)}) async-start(bf16[16,2,2176]{2,1,0:T(2,128)(2,1)} %pack.1), calls=%async_computation | async-start | bytes 278528 | tf_op jit(solution)/shard_map/all_to_all | solution.py:226
  9.6 4.0 %build.1 = (bf16[2,1024,512]{2,1,0:T(8,128)(2,1)S(1)}, f32[16,512]{1,0:T(8,128)S(1)}) custom-call(s32[64,1024]{1,0:T(8,128)} %bitcast.10, f32[64,16,256]{2,1,0:T(8,128)} %bitcast.9, bf16[1024,1024]{1,0:T(8,128)(2,1)} %residual_hbm.1), custom_call_target="tpu_custom_call" | custom-call | flops 16777216 | bytes 4194304 | tf_op jit(solution)/shard_map/build/pallas_call | solution.py:131
  13.6 1.7 %all-to-all-done.visiting_ref = bf16[16,2,2176]{2,1,0:T(2,128)(2,1)S(1)} async-done(((bf16[16,2,2176]{2,1,0:T(2,128)(2,1)}), bf16[16,2,2176]{2,1,0:T(2,128)(2,1)S(1)}, u32[]{:S(2)}, u32[]{:S(2)}) %all-to-all-start) | async-done | bytes 139296 | tf_op jit(solution)/shard_map/all_to_all | solution.py:226
  15.3 0.6 %count.1 = f32[2,16,1,128]{3,2,1,0:T(1,128)S(1)} custom-call(bf16[16,2,2176]{2,1,0:T(2,128)(2,1)S(1)} %all-to-all-done.visiting_ref, bf16[2,1024,512]{2,1,0:T(8,128)(2,1)S(1)} %get-tuple-element.6.values_ref, f32[16,512]{1,0:T(8,128)S(1)} %get-tuple-element.7.norms_ref), custom_call_target="tpu_custom_call" | custom-call | flops 134217728 | bytes 2097152 | tf_op jit(solution)/shard_map/count/pallas_call | solution.py:230
  16.0 10.1 %all_to_all.10 = f32[32,1,128]{2,1,0:T(1,128)S(1)} all-to-all(f32[32,1,128]{2,1,0:T(1,128)S(1)} %bitcast.7), channel_id=1, replica_groups=mesh['pb'=4,'db'=8] {'pb','db'}, dimensions={0} | all-to-all | bytes 32768 | tf_op jit(solution)/shard_map/all_to_all | solution.py:242
  26.1 0.7 %finish.1 = (f32[3,4]{1,0:T(4,128)}, f32[1,3]{1,0:T(1,128)}) custom-call(f32[4,8,1,128]{3,2,1,0:T(1,128)S(1)} %bitcast.8), custom_call_target="tpu_custom_call" | custom-call | tf_op jit(solution)/shard_map/finish/pallas_call | solution.py:243
Async XLA Ops:
  2.0 13.3 %all-to-all-start = ((bf16[16,2,2176]{2,1,0:T(2,128)(2,1)}), bf16[16,2,2176]{2,1,0:T(2,128)(2,1)S(1)}, u32[]{:S(2)}, u32[]{:S(2)}) async-start(bf16[16,2,2176]{2,1,0:T(2,128)(2,1)} %pack.1), calls=%async_computation | async-start | bytes 278528 | tf_op jit(solution)/shard_map/all_to_all | solution.py:226

commit v7 on v6

--- a/solution.py
+++ b/solution.py
@@ -221,7 +221,7 @@
     assert 3 * count + 3 <= LANES
 
     stride = senders // 2 - 1 if math.gcd(senders // 2 - 1, senders) == 1 else 1
-    order = [(senders - shards // 2 - 1 + stride * i) % senders for i in range(senders)]
+    order = [(senders - shards // 2 + stride * i) % senders for i in range(senders)]
     groups = [[first + at for at in order] for first in range(0, devices, senders)]
     visiting = lax.all_to_all(
         pack(queries, ranks, senders, lines), ("pb", "db"), 0, 0, axis_index_groups=groups

time: 27.2 us -> 27.2 us (level)
  no operation moved by 1% of the time
where the time goes in v7:
time: 27.2 us; the launch traced here: 26.8 us
  blocking collectives  10.1 us (37%)
  starting transfers between devices  7.62 us (28%)
  Pallas kernels  6.65 us (24%)
  waiting for transfers between devices  1.7 us (6%)
  between operations  0.65 us (2%)
    all_to_all x1, blocking collectives, per_device(): lax.all_to_all(partial_sums.reshape(devices, 1, LANES), ('pb', 'db'), 0, 0)  10.1 us
    all_to_all x1, starting transfers between devices, per_device(): lax.all_to_all(pack(queries, ranks, senders, lines), ('pb', 'db'), 0, 0,...  7.62 us
    pallas_call x1, Pallas kernels, build(): pl.pallas_call(build_kernel, in_specs=[pl.BlockSpec(memory_space=pltpu.HB...  3.96 us
    all_to_all x1, waiting for transfers between devices, per_device(): lax.all_to_all(pack(queries, ranks, senders, lines), ('pb', 'db'), 0, 0,...  1.7 us
    pallas_call x1, Pallas kernels, pack(): pl.pallas_call(pack_kernel, in_specs=[pl.BlockSpec(memory_space=pltpu.HBM...  1.37 us
    pallas_call x1, Pallas kernels, per_device(): pl.pallas_call(functools.partial(finish_kernel, fold, rows * senders, cou...  0.67 us
    pallas_call x1, Pallas kernels, per_device(): pl.pallas_call(functools.partial(count_kernel, order), out_shape=jax.Shap...  0.64 us
  transfers between devices with their start and end apart: 1, of which 1 were waited for; matrix products, arithmetic and copies ran while one was open for 0% of the time, Pallas kernels for 15%

profile of v7, /device:TPU:0, one launch (start us, length us, event | category | flops | bytes accessed | tf_op | source)
XLA Modules:
  0.0 26.8 jit_solution(8473967132775439758)
XLA Ops:
  0.6 1.4 %pack.1 = bf16[16,2,2176]{2,1,0:T(2,128)(2,1)} custom-call(bf16[4,1024]{1,0:T(4,128)(2,1)} %queries_hbm.1, s32[4]{0:T(128)} %ranks_hbm.1), custom_call_target="tpu_custom_call" | custom-call | tf_op jit(solution)/shard_map/pack/pallas_call | solution.py:45
  2.0 7.6 %all-to-all-start = ((bf16[16,2,2176]{2,1,0:T(2,128)(2,1)}), bf16[16,2,2176]{2,1,0:T(2,128)(2,1)S(1)}, u32[]{:S(2)}, u32[]{:S(2)}) async-start(bf16[16,2,2176]{2,1,0:T(2,128)(2,1)} %pack.1), calls=%async_computation | async-start | bytes 278528 | tf_op jit(solution)/shard_map/all_to_all | solution.py:226
  9.6 4.0 %build.1 = (bf16[2,1024,512]{2,1,0:T(8,128)(2,1)S(1)}, f32[16,512]{1,0:T(8,128)S(1)}) custom-call(s32[64,1024]{1,0:T(8,128)} %bitcast.10, f32[64,16,256]{2,1,0:T(8,128)} %bitcast.9, bf16[1024,1024]{1,0:T(8,128)(2,1)} %residual_hbm.1), custom_call_target="tpu_custom_call" | custom-call | flops 16777216 | bytes 4194304 | tf_op jit(solution)/shard_map/build/pallas_call | solution.py:131
  13.6 1.7 %all-to-all-done.visiting_ref = bf16[16,2,2176]{2,1,0:T(2,128)(2,1)S(1)} async-done(((bf16[16,2,2176]{2,1,0:T(2,128)(2,1)}), bf16[16,2,2176]{2,1,0:T(2,128)(2,1)S(1)}, u32[]{:S(2)}, u32[]{:S(2)}) %all-to-all-start) | async-done | bytes 139296 | tf_op jit(solution)/shard_map/all_to_all | solution.py:226
  15.3 0.6 %count.1 = f32[2,16,1,128]{3,2,1,0:T(1,128)S(1)} custom-call(bf16[16,2,2176]{2,1,0:T(2,128)(2,1)S(1)} %all-to-all-done.visiting_ref, bf16[2,1024,512]{2,1,0:T(8,128)(2,1)S(1)} %get-tuple-element.6.values_ref, f32[16,512]{1,0:T(8,128)S(1)} %get-tuple-element.7.norms_ref), custom_call_target="tpu_custom_call" | custom-call | flops 134217728 | bytes 2097152 | tf_op jit(solution)/shard_map/count/pallas_call | solution.py:230
  15.9 10.1 %all_to_all.10 = f32[32,1,128]{2,1,0:T(1,128)S(1)} all-to-all(f32[32,1,128]{2,1,0:T(1,128)S(1)} %bitcast.7), channel_id=1, replica_groups=mesh['pb'=4,'db'=8] {'pb','db'}, dimensions={0} | all-to-all | bytes 32768 | tf_op jit(solution)/shard_map/all_to_all | solution.py:242
  26.1 0.7 %finish.1 = (f32[3,4]{1,0:T(4,128)}, f32[1,3]{1,0:T(1,128)}) custom-call(f32[4,8,1,128]{3,2,1,0:T(1,128)S(1)} %bitcast.8), custom_call_target="tpu_custom_call" | custom-call | tf_op jit(solution)/shard_map/finish/pallas_call | solution.py:243
Async XLA Ops:
  2.0 13.3 %all-to-all-start = ((bf16[16,2,2176]{2,1,0:T(2,128)(2,1)}), bf16[16,2,2176]{2,1,0:T(2,128)(2,1)S(1)}, u32[]{:S(2)}, u32[]{:S(2)}) async-start(bf16[16,2,2176]{2,1,0:T(2,128)(2,1)} %pack.1), calls=%async_computation | async-start | bytes 278528 | tf_op jit(solution)/shard_map/all_to_all | solution.py:226
